TPU v7x, 256 devices: a whole 4x4x8 slice. The times are simulated.
256 devices in a mesh: pt: 8 (over x, y_lo), tp: 32 (over y_hi, z, core).
Axes of the slice: x: 4, y: 4 (y_hi: 2, y_lo: 2; y = y_hi * 2 + y_lo), z: 8, core: 2. Of those that a mesh axis runs over, the one named last changes fastest.
Arguments:
- tokens: bfloat16 [4096, 4096], P('pt', 'tp'), may hold values from -6 to 6
- t_values: float32 [8], replicated, may hold values from 0.05 to 0.95
- gate_start: bfloat16 [4096, 14336], P('pt', 'tp'), may hold values from -0.09375 to 0.09375
- gate_bend: bfloat16 [4096, 14336], P('pt', 'tp'), may hold values from -0.1875 to 0.1875
- gate_end: bfloat16 [4096, 14336], P('pt', 'tp'), may hold values from -0.09375 to 0.09375
- up_start: bfloat16 [4096, 14336], P('pt', 'tp'), may hold values from -0.09375 to 0.09375
- up_bend: bfloat16 [4096, 14336], P('pt', 'tp'), may hold values from -0.1875 to 0.1875
- up_end: bfloat16 [4096, 14336], P('pt', 'tp'), may hold values from -0.09375 to 0.09375
- hidden_grad: bfloat16 [4096, 14336], P('pt', 'tp'), may hold values from -6 to 6
Outputs:
- hidden: bfloat16 [4096, 14336], P('pt', 'tp')
- input_grad: bfloat16 [4096, 4096], P('pt', 'tp')
- gate_bend_grad: float32 [4096, 14336], P('pt', 'tp')
- up_bend_grad: float32 [4096, 14336], P('pt', 'tp')
All inputs are finite; a program needn't handle non-finite values.
Results may differ from a plain program's by a relative error of at most 0.014.
Values may be sent and summed in bfloat16 or wider, within the bound.
A program may use at most 128 MiB of HBM per device.

v0:
```python
import jax
import jax.numpy as jnp
from jax import lax
from jax.sharding import PartitionSpec as P


def in_one_piece(arrays, axis, split_dim, concat_dim, along):
    both = jnp.concatenate(arrays, axis=along)
    filled, at, finished = (
        lax.all_to_all(both, axis, split_axis=split_dim, concat_axis=concat_dim, tiled=True),
        0,
        [],
    )
    for a in arrays:
        finished.append(lax.slice_in_dim(filled, at, at + a.shape[along], axis=along))
        at += a.shape[along]
    return tuple(finished)


def cut_along(array, dim, size):
    before, after = (array.shape[:dim], array.shape[dim + 1 :])
    return jnp.moveaxis(array.reshape(*before, size, -1, *after), dim, 0)


def summed_on_arrival(array, axis, dim):
    parts = cut_along(array, dim, lax.axis_size(axis))
    arrived = lax.all_to_all(parts, axis, split_axis=0, concat_axis=0, tiled=True)
    return arrived.astype(jnp.float32).sum(axis=0)


def in_one_piece_2(arrays, axis, dim, along):
    ends, at = ([], 0)
    for a in arrays[:-1]:
        at += a.shape[along]
        ends.append(at)
    both = jnp.concatenate(arrays, axis=along)
    return tuple(
        jnp.split(lax.psum_scatter(both, axis, scatter_dimension=dim, tiled=True), ends, axis=along)
    )


def blend_all(first, middle, last, start, bend, end):
    mixed = (
        first[:, None, None] * start.astype(jnp.float32)[None]
        + middle[:, None, None] * bend.astype(jnp.float32)[None]
        + last[:, None, None] * end.astype(jnp.float32)[None]
    )
    return mixed.astype(jnp.bfloat16)


def per_device(
    tokens, t_values, gate_start, gate_bend, gate_end, up_start, up_bend, up_end, hidden_grad
):
    mine = lax.axis_index("pt")
    first = (1.0 - t_values) ** 2
    middle = 2.0 * t_values * (1.0 - t_values)
    last = t_values * t_values
    gate_parts = blend_all(first, middle, last, gate_start, gate_bend, gate_end)
    up_parts = blend_all(first, middle, last, up_start, up_bend, up_end)
    gate_full, up_full = in_one_piece((gate_parts, up_parts), "pt", 0, 1, 2)
    gate_w = gate_full[0]
    up_w = up_full[0]
    whole = lax.all_gather(tokens, "tp", axis=1, tiled=True)
    gate = jnp.dot(whole, gate_w, preferred_element_type=jnp.float32)
    up = jnp.dot(whole, up_w, preferred_element_type=jnp.float32)
    sig = jax.nn.sigmoid(gate)
    act = gate * sig
    hidden = (act * up).astype(jnp.bfloat16)
    cotf = hidden_grad.astype(jnp.float32)
    d_up = cotf * act
    d_gate = cotf * up * sig * (1.0 + gate * (1.0 - sig))
    d_gate_b = d_gate.astype(jnp.bfloat16)
    d_up_b = d_up.astype(jnp.bfloat16)
    weight_here = lax.dynamic_index_in_dim(middle, mine, 0, keepdims=False)
    scaled_gate = (weight_here * d_gate).astype(jnp.bfloat16)
    scaled_up = (weight_here * d_up).astype(jnp.bfloat16)
    part_gate = lax.dot_general(
        gate_w, d_gate_b, (((1,), (1,)), ((), ())), preferred_element_type=jnp.float32
    )
    part_up = lax.dot_general(
        up_w, d_up_b, (((1,), (1,)), ((), ())), preferred_element_type=jnp.float32
    )
    input_cols = summed_on_arrival((part_gate + part_up).astype(jnp.bfloat16), "tp", 0)
    input_grad = input_cols.T.astype(jnp.bfloat16)
    full_gate = lax.dot_general(
        whole, scaled_gate, (((0,), (0,)), ((), ())), preferred_element_type=jnp.float32
    )
    full_up = lax.dot_general(
        whole, scaled_up, (((0,), (0,)), ((), ())), preferred_element_type=jnp.float32
    )
    gate_grad, up_grad = tuple(
        (
            part.astype(jnp.float32)
            for part in in_one_piece_2(
                (full_gate.astype(jnp.bfloat16), full_up.astype(jnp.bfloat16)), "pt", 0, 1
            )
        )
    )
    return (hidden, input_grad, gate_grad, up_grad)


def solution(mesh):
    return jax.shard_map(
        per_device,
        mesh=mesh,
        in_specs=(
            P("pt", "tp"),
            P(),
            P("pt", "tp"),
            P("pt", "tp"),
            P("pt", "tp"),
            P("pt", "tp"),
            P("pt", "tp"),
            P("pt", "tp"),
            P("pt", "tp"),
        ),
        out_specs=(P("pt", "tp"), P("pt", "tp"), P("pt", "tp"), P("pt", "tp")),
        check_vma=False,
    )
```

profile of v0, /device:TPU:3, one launch (start us, length us, event | category | flops | bytes accessed | tf_op | source)
XLA Modules:
  0.0 381.9 jit_solution(16434651966500397295)
XLA Ops:
  7.2 0.0 copy-start.1
  7.2 0.0 all-gather.2.cloned.1.call-start
  7.2 0.7 all-gather.2.cloned.1.call-update
  7.9 1.2 copy.19
  9.1 1.2 copy.20
  10.4 1.2 copy.21
  11.6 2.2 copy.22
  13.8 2.2 copy.23
  16.0 2.3 copy.24
  18.3 0.0 copy-done.1
  18.3 6.8 %add_convert_fusion.2 = (bf16[8,512,448]{2,1,0:T(8,128)(2,1)}, bf16[8,512,448]{2,1,0:T(8,128)(2,1)}) fusion(f32[512,448]{1,0:T(8,128)S(1)} %copy.21, f32[8]{0:T(128)S(1)} %get-tuple-element.13, f32[512,448]{1,0:T(8,128)S(1)} %copy.20, f32[8]{0:T(128)S(1)} %get-tuple-element.14, f32[512,448]{1,0:T(8,128)S(1)} %copy.19, f32[8]{0:T(128)S(1)} %get-tuple-element.12, ...), kind=kLoop, calls=%fused_computation.2 | loop fusion | flops 22020096 | bytes 12845152 | tf_op jit(solution)/shard_map/convert_element_type | solution.py:48
  25.1 9.4 %pad_maximum_fusion = bf16[8,512,896]{2,1,0:T(8,128)(2,1)} fusion(bf16[8,512,448]{2,1,0:T(8,128)(2,1)} %get-tuple-element.11, bf16[8,512,448]{2,1,0:T(8,128)(2,1)} %get-tuple-element.10), kind=kLoop, calls=%fused_computation.3 | loop fusion | flops 14680064 | bytes 14680064 | tf_op jit(solution)/shard_map/concatenate | solution.py:8
  34.5 5.3 %all-to-all-start = ((bf16[8,512,896]{2,1,0:T(8,128)(2,1)}), bf16[8,512,896]{2,1,0:T(8,128)(2,1)}, u32[]{:S(2)}, u32[]{:S(2)}) async-start(bf16[8,512,896]{2,1,0:T(8,128)(2,1)} %pad_maximum_fusion), calls=%async_computation | async-start | bytes 14680064 | tf_op jit(solution)/shard_map/all_to_all | solution.py:10
  39.8 0.0 reduce-scatter.2.cloned.1.call-start
  39.8 0.6 dynamic_slice.4
  40.4 96.8 %all-to-all-done = bf16[8,512,896]{2,1,0:T(8,128)(2,1)} async-done(((bf16[8,512,896]{2,1,0:T(8,128)(2,1)}), bf16[8,512,896]{2,1,0:T(8,128)(2,1)}, u32[]{:S(2)}, u32[]{:S(2)}) %all-to-all-start) | async-done | bytes 7340064 | tf_op jit(solution)/shard_map/all_to_all | solution.py:10
  137.1 13.7 %all-gather.2.cloned.1.call-done = bf16[512,4096]{1,0:T(8,128)(2,1)} async-done(((bf16[512,128]{1,0:T(8,128)(2,1)}), bf16[512,4096]{1,0:T(8,128)(2,1)}) %all-gather.2.cloned.1.call-update) | async-done | bytes 4194320 | tf_op jit(solution)/shard_map/all_gather | solution.py:63
  150.8 0.0 copy-start.2
  150.8 6.1 %fusion.6 = f32[512,448]{0,1:T(8,128)S(1)} fusion(bf16[512,4096]{1,0:T(8,128)(2,1)} %all-gather.2.cloned.1.call-done, bf16[1,4096,896]{2,1,0:T(8,128)(2,1)} %bitcast), kind=kOutput, calls=%fused_computation.15 | convolution fusion | flops 1879048192 | bytes 9306112 | tf_op jit(solution)/shard_map/dot_general | solution.py:64
  157.0 0.0 copy-done.2
  157.0 0.0 copy-start
  157.0 6.7 %multiply_convert_fusion.2 = (bf16[512,448]{0,1:T(8,128)(2,1)}, f32[512,448]{0,1:T(8,128)S(1)}) fusion(f32[512,448]{0,1:T(8,128)S(1)} %fusion.6, bf16[512,4096]{1,0:T(8,128)(2,1)S(1)} %copy-done.2, bf16[1,4096,896]{2,1,0:T(8,128)(2,1)} %bitcast), kind=kOutput, calls=%fused_computation.22 | convolution fusion | flops 1880424448 | bytes 10682368 | tf_op jit(solution)/shard_map/dot_general | solution.py:65
  163.7 0.0 copy-start.3
  163.7 0.0 copy-done
  163.7 2.8 fusion.1
  166.6 0.0 copy-done.3
  166.6 4.8 %fusion = bf16[4096,448]{0,1:T(8,128)(2,1)} fusion(bf16[512,4096]{1,0:T(8,128)(2,1)S(1)} %copy-done.2, f32[]{:T(128)} %bitcast.7, f32[512,448]{0,1:T(8,128)S(1)} %get-tuple-element.16, bf16[512,448]{0,1:T(8,128)(2,1)S(1)} %copy-done, f32[512,448]{0,1:T(8,128)S(1)} %fusion.6), kind=kOutput, calls=%fused_computation.7 | convolution fusion | flops 1883635712 | bytes 10158084 | tf_op jit(solution)/shard_map/dot_general | solution.py:85
  171.4 6.3 %pad_maximum_fusion.1 = bf16[4096,896]{0,1:T(8,128)(2,1)} fusion(bf16[4096,448]{0,1:T(8,128)(2,1)S(1)} %fusion.1, bf16[4096,448]{0,1:T(8,128)(2,1)} %fusion), kind=kLoop, calls=%fused_computation.4 | loop fusion | flops 14680064 | bytes 14680064 | tf_op jit(solution)/shard_map/concatenate | solution.py:36
  177.7 0.0 copy-start.4
  177.7 0.0 reduce-scatter.2.cloned.1.call-update
  177.7 1.2 copy-done.4
  178.9 5.0 %fusion.2 = f32[4096,512]{1,0:T(8,128)S(1)} fusion(bf16[1,4096,896]{2,1,0:T(8,128)(2,1)} %bitcast, f32[512,448]{0,1:T(8,128)S(1)} %copy-done.4, bf16[512,448]{0,1:T(8,128)(2,1)S(1)} %copy-done, f32[512,448]{0,1:T(8,128)S(1)} %fusion.6), kind=kOutput, calls=%fused_computation.11 | convolution fusion | flops 1881571328 | bytes 14876672 | tf_op jit(solution)/shard_map/dot_general | solution.py:77
  183.8 4.8 %add_convert_fusion = bf16[4096,512]{1,0:T(8,128)(2,1)S(1)} fusion(f32[4096,512]{1,0:T(8,128)S(1)} %fusion.2, bf16[1,4096,896]{2,1,0:T(8,128)(2,1)} %bitcast, bf16[512,448]{0,1:T(8,128)(2,1)S(1)} %copy-done, f32[512,448]{0,1:T(8,128)S(1)} %fusion.6), kind=kOutput, calls=%fused_computation | convolution fusion | flops 1884848128 | bytes 18153472 | tf_op jit(solution)/shard_map/dot_general | solution.py:80
  188.7 100.8 %all_to_all.17 = bf16[32,128,512]{2,1,0:T(8,128)(2,1)} all-to-all(bf16[32,128,512]{2,1,0:T(8,128)(2,1)S(1)} %bitcast.30), channel_id=1, replica_groups=mesh['pt'=8,'tp'=32] {'tp'}, dimensions={0} | all-to-all | bytes 8388608 | tf_op jit(solution)/shard_map/all_to_all | solution.py:27
  289.4 2.8 reduce_sum.12
  292.2 0.8 copy.25
  293.0 79.4 %reduce-scatter.2.cloned.1.call-done = bf16[512,896]{0,1:T(8,128)(2,1)} async-done(((bf16[4096,896]{0,1:T(8,128)(2,1)}), bf16[512,896]{0,1:T(8,128)(2,1)}) %reduce-scatter.2.cloned.1.call-update) | async-done | bytes 917520 | tf_op jit(solution)/shard_map/reduce_scatter | solution.py:38
  372.4 2.6 slice_convert_fusion
  (1 shorter events, 0.0 us)
Async XLA Ops:
  7.2 11.1 %copy-start.1 = (f32[8]{0:T(128)S(1)}, f32[8]{0:T(128)}, u32[]{:S(2)}) copy-start(f32[8]{0:T(128)} %param.10) | copy-start | bytes 100
  7.2 143.7 %all-gather.2.cloned.1.call-start = ((), (), s32[]{:S(2)}) async-start(), calls=%async_computation.3 | async-start | bytes 4325376 | tf_op jit(solution)/shard_map/all_gather | solution.py:63
  34.5 102.6 %all-to-all-start = ((bf16[8,512,896]{2,1,0:T(8,128)(2,1)}), bf16[8,512,896]{2,1,0:T(8,128)(2,1)}, u32[]{:S(2)}, u32[]{:S(2)}) async-start(bf16[8,512,896]{2,1,0:T(8,128)(2,1)} %pad_maximum_fusion), calls=%async_computation | async-start | bytes 14680064 | tf_op jit(solution)/shard_map/all_to_all | solution.py:10
  39.8 332.6 %reduce-scatter.2.cloned.1.call-start = ((), (), s32[]{:S(2)}) async-start(), calls=%async_computation.4 | async-start | bytes 8257536 | tf_op jit(solution)/shard_map/reduce_scatter | solution.py:38
  150.8 6.1 %copy-start.2 = (bf16[512,4096]{1,0:T(8,128)(2,1)S(1)}, bf16[512,4096]{1,0:T(8,128)(2,1)}, u32[]{:S(2)}) copy-start(bf16[512,4096]{1,0:T(8,128)(2,1)} %all-gather.2.cloned.1.call-done) | copy-start | bytes 12582916
  157.0 6.8 %copy-start = (bf16[512,448]{0,1:T(8,128)(2,1)S(1)}, bf16[512,448]{0,1:T(8,128)(2,1)}, u32[]{:S(2)}) copy-start(bf16[512,448]{0,1:T(8,128)(2,1)} %param.17) | copy-start | bytes 1376260
  163.7 2.8 copy-start.3
  177.7 1.2 copy-start.4
Sparse Core Ops, SparseCore 0:
  10.5 140.2 all-gather.1
  177.8 194.4 reduce-scatter.1
where the time goes:
time: 383 us; the launch traced here: 382 us
  waiting for transfers between devices  191 us (50%)
  blocking collectives  101 us (26%)
  matrix products  30.3 us (8%)
  other arithmetic  28 us (7%)
  between operations  14.1 us (4%)
  local copies, waits for them, and re-layouts  12.9 us (3%)
  starting transfers between devices  5.32 us (1%)
    all_to_all x1, blocking collectives, summed_on_arrival(): lax.all_to_all(parts, axis, split_axis=0, concat_axis=0, tiled=True)  101 us
    all_to_all x1, waiting for transfers between devices, in_one_piece(): lax.all_to_all(both, axis, split_axis=split_dim, concat_axis=concat_dim,...  96.8 us
    reduce_scatter x1, waiting for transfers between devices, in_one_piece_2(): lax.psum_scatter(both, axis, scatter_dimension=dim, tiled=True)  79.4 us
    all_gather x1, waiting for transfers between devices, per_device(): whole = lax.all_gather(tokens, 'tp', axis=1, tiled=True)  13.7 us
    concatenate x1, other arithmetic, in_one_piece(): both = jnp.concatenate(arrays, axis=along)  9.42 us
  transfers between devices with their start and end apart: 3, of which 3 were waited for; matrix products, arithmetic and copies ran while one was open for 11% of the time, Pallas kernels for 0%

commit v1 on v0

v1 whole, which is shorter than its diff:
```python
import functools

import jax
import jax.numpy as jnp
from jax import lax
from jax.experimental import pallas as pl
from jax.experimental.pallas import tpu as pltpu
from jax.sharding import PartitionSpec as P

MESH = pl.DeviceIdType.MESH
F32, BF = jnp.float32, jnp.bfloat16

ROWS = ((0, 256), (256, 256))
COLS = ((0, 256), (256, 256), (512, 256), (768, 128))
CELLS = ((0, 0), (1, 0), (0, 1), (1, 1), (0, 2), (0, 3), (1, 2), (1, 3))
NH, NF, NC = len(ROWS), len(COLS), len(CELLS)
HOPS = ((4, 3), (3, 4))
KORDER = (4, 3, 5, 2, 6, 1, 7, 0)


def div(a, b):
    return lax.div(a, jnp.int32(b))


def rem(a, b):
    return lax.rem(a, jnp.int32(b))


def mul_of(a, b):
    return pl.multiple_of(a, b)


def kernel(
    tok, ts, gs, gb, ge, us, ub, ue, hg,
    hid, ig, gg, ug,
    xbuf, xt, rawp, rawm, wbuf, fbuf, sbuf, r1, r2, dbuf, dwown, ysend, yrecv,
    dxo, dxs, dxr, zs, zr, fs, fr, ta, tb, hgm,
    p0_s, p0_r, tz_s, tz_r, td_s, td_r, w_s, w_r, x_s, x_r, y_s, y_r,
    dd_s, dd_r, dz_s, dz_r, f_s, f_r,
):
    p, t = lax.axis_index("pt"), lax.axis_index("tp")
    x, g = div(p, 2), rem(p, 2)
    yh, z, c = div(t, 16), rem(div(t, 2), 8), rem(t, 2)
    xp, xm, x2 = rem(x + 1, 4), rem(x + 3, 4), rem(x + 2, 4)
    dev_xp, dev_xm = (2 * xp + g, t), (2 * xm + g, t)
    dev_y = (2 * x + (1 - g), t)
    dev_c = (p, yh * 16 + z * 2 + (1 - c))
    dev_z = ((p, yh * 16 + rem(z + 1, 8) * 2 + c), (p, yh * 16 + rem(z + 7, 8) * 2 + c))
    pp, pq = 2 * div(t, 8) + g, 8 * x + rem(t, 8)
    t2 = rem(t + 16, 32)
    dev_p = (pp, pq)
    dev_d2 = (pp, rem(pq + 16, 32))
    dev_s2 = (2 * div(t2, 8) + g, 8 * x + rem(t, 8))
    away = div(t, 8) != x

    barrier = pltpu.get_barrier_semaphore()
    for dev in (dev_xp, dev_xm, dev_y, dev_c, dev_z[0], dev_z[1], dev_d2, dev_s2):
        pl.semaphore_signal(barrier, inc=1, device_id=dev, device_id_type=MESH)

    @pl.when(away)
    def _():
        pl.semaphore_signal(barrier, inc=1, device_id=dev_p, device_id_type=MESH)

    pl.semaphore_wait(barrier, 8 + away.astype(jnp.int32))

    sent = []

    def rc(src, dst, ss, rs, dev):
        return pltpu.make_async_remote_copy(
            src_ref=src, dst_ref=dst, send_sem=ss, recv_sem=rs, device_id=dev, device_id_type=MESH
        )

    def send(src, dst, ss, rs, dev):
        d = rc(src, dst, ss, rs, dev)
        d.start()
        sent.append(d)

    def arrived(dst, ss, rs, dev):
        rc(dst, dst, ss, rs, dev).wait_recv()

    def block(tidx, h):
        r0, rn = ROWS[h]
        row = mul_of(512 * div(tidx, 8) + r0, 32)
        return xbuf.at[pl.ds(row, rn), pl.ds(mul_of(128 * rem(tidx, 8), 128), 128)]

    def tblock(z0, piece, cc, h):
        return block(rem(yh + piece, 2) * 16 + z0 * 2 + cc, h)

    def tok_scatter(h):
        r0, rn = ROWS[h]
        mine = tok.at[pl.ds(r0, rn), :]

        @pl.when(away)
        def _():
            rc(mine, block(pq, h), p0_s.at[h, 0], p0_r.at[h, 0], dev_p).start()

        send(mine, block(pq, h), p0_s.at[h, 1], p0_r.at[h, 1], dev_d2)

        @pl.when(jnp.logical_not(away))
        def _():
            block(t, h)[...] = tok[pl.ds(r0, rn), :]

    def tok_arrive(h, piece):
        if piece == 0:
            @pl.when(away)
            def _():
                arrived(block(t, h), p0_s.at[h, 0], p0_r.at[h, 0], dev_p)
        else:
            arrived(block(t2, h), p0_s.at[h, 1], p0_r.at[h, 1], dev_d2)

    def z_at(direction, s):
        return rem(z + 8 - s, 8) if direction == 0 else rem(z + s, 8)

    def to_sibling(h, piece, direction, s):
        slot = piece * 8 + (s if direction == 0 else (0 if s == 0 else HOPS[0][piece] + s))
        b = tblock(z_at(direction, s), piece, c, h)
        send(b, b, td_s.at[h, slot], td_r.at[h, slot], dev_c)

    def tok_step(h, s):
        for piece in (0, 1):
            if s == 0:
                tok_arrive(h, piece)
            for direction in (0, 1):
                if s > HOPS[direction][piece]:
                    continue
                b = tblock(z_at(direction, s), piece, c, h)
                if s > 0:
                    arrived(b, tz_s.at[h, direction, piece, s - 1], tz_r.at[h, direction, piece, s - 1],
                            dev_z[1 - direction])
                if s < HOPS[direction][piece]:
                    send(b, b, tz_s.at[h, direction, piece, s], tz_r.at[h, direction, piece, s], dev_z[direction])
                if s > 0 or direction == 0:
                    to_sibling(h, piece, direction, s)

    def tok_done(h):
        for piece in (0, 1):
            for direction in (0, 1):
                for s in range(HOPS[direction][piece] + 1):
                    if s == 0 and direction == 1:
                        continue
                    slot = piece * 8 + (s if direction == 0 else HOPS[0][piece] + s)
                    arrived(tblock(z_at(direction, s), piece, 1 - c, h), td_s.at[h, slot], td_r.at[h, slot], dev_c)

    def tok_transpose(h):
        r0, rn = ROWS[h]

        def one(i, _):
            jr, cb = div(i, 8), rem(i, 8)
            v = xbuf[pl.ds(mul_of(512 * jr + r0, 32), rn), pl.ds(mul_of(128 * cb, 128), 128)]
            xt[jr, pl.ds(mul_of(128 * cb, 128), 128), pl.ds(r0, rn)] = v.T
            return 0

        lax.fori_loop(0, 32, one, 0)

    raws = ((gs, us), (gb, ub), (ge, ue))

    def w_send(f):
        for m in range(3):
            if f < 3:
                for k in range(2):
                    i = f * 6 + m * 2 + k
                    send(raws[m][k].at[:, pl.ds(128 * f, 128)], rawp.at[i], w_s.at[i], w_r.at[i], dev_y)
            else:
                i = 18 + m
                send(rawm.at[m], rawp.at[i], w_s.at[i], w_r.at[i], dev_y)

    def w_arrive(f):
        for i in range(f * 6, f * 6 + 6) if f < 3 else range(18, 21):
            arrived(rawp.at[i], w_s.at[i], w_r.at[i], dev_y)

    lane = lax.broadcasted_iota(jnp.int32, (128, 128), 1)

    def pack():
        for m in range(3):
            ta[:, 0:64] = raws[m][0][:, 384:448].astype(F32)
            tb[:, 0:64] = raws[m][1][:, 384:448].astype(F32)

            def one(i, _):
                r = pl.ds(mul_of(i * 128, 128), 128)
                rawm[m, r, :] = jnp.where(lane < 64, ta[r, :], pltpu.roll(tb[r, :], 64, 1)).astype(BF)
                return 0

            lax.fori_loop(0, 4, one, 0)

    ta[...] = jnp.zeros_like(ta)
    tb[...] = jnp.zeros_like(tb)
    hgm[...] = jnp.zeros_like(hgm)
    hgm[:, 0:64] = hg[:, 384:448].astype(F32)

    tv = [ts[2 * j + g] for j in range(4)]
    coef = [((1.0 - v) * (1.0 - v), 2.0 * v * (1.0 - v), v * v) for v in tv]

    def blend(f, own):
        side = g if own else 1 - g

        def one(i, _):
            r = pl.ds(mul_of(i * 64, 64), 64)
            w = pl.ds(mul_of(side * 512 + i * 64, 64), 64)
            for k in range(2 if f < 3 else 1):
                if f < 3:
                    v = [(raws[m][k][r, 128 * f:128 * f + 128] if own else rawp[f * 6 + m * 2 + k, r, :])
                         for m in range(3)]
                else:
                    v = [(rawm[m, r, :] if own else rawp[18 + m, r, :]) for m in range(3)]
                v = [a.astype(F32) for a in v]
                c0 = COLS[f][0] + 128 * k
                for j in range(4):
                    b0, b1, b2 = coef[j]
                    wbuf[j, w, c0:c0 + 128] = (b0 * v[0] + b1 * v[1] + b2 * v[2]).astype(BF)
            return 0

        lax.fori_loop(0, 8, one, 0)

    def cell(i):
        h, f = CELLS[i]
        return ROWS[h] + COLS[f] + (f,)

    def at(ref, i, lo=0.0, hi=1.0):
        r0, rn, c0, cn, _ = cell(i)
        return ref.at[pl.ds(r0 + int(rn * lo), int(rn * (hi - lo))), pl.ds(c0, cn)]

    def forward(i):
        r0, rn, c0, cn, _ = cell(i)

        def one(k, _):
            jr = rem(x + k, 4)
            fbuf[k, r0:r0 + rn, c0:c0 + cn] = jnp.dot(
                xbuf[pl.ds(mul_of(512 * jr + r0, 32), rn), :], wbuf[jr, :, c0:c0 + cn],
                preferred_element_type=F32)
            return 0

        lax.fori_loop(0, 4, one, 0)
        sbuf[0, r0:r0 + rn, c0:c0 + cn] = fbuf[2, r0:r0 + rn, c0:c0 + cn].astype(BF)
        send(at(sbuf.at[0], i, 0.0, 0.5), at(r1, i, 0.0, 0.5), x_s.at[i, 0], x_r.at[i, 0], dev_xp)
        send(at(sbuf.at[0], i, 0.5, 1.0), at(r1, i, 0.5, 1.0), x_s.at[i, 1], x_r.at[i, 1], dev_xm)

    def reduce(i):
        r0, rn, c0, cn, _ = cell(i)
        n = rn // 2
        a, b, cs = slice(r0, r0 + n), slice(r0 + n, r0 + rn), slice(c0, c0 + cn)
        arrived(at(r1, i, 0.0, 0.5), x_s.at[i, 0], x_r.at[i, 0], dev_xm)
        sbuf[1, a, cs] = (fbuf[1, a, cs] + r1[a, cs].astype(F32)).astype(BF)
        sbuf[1, b, cs] = fbuf[1, b, cs].astype(BF)
        send(at(sbuf.at[1], i), at(r2.at[0], i), x_s.at[i, 2], x_r.at[i, 2], dev_xp)
        arrived(at(r1, i, 0.5, 1.0), x_s.at[i, 1], x_r.at[i, 1], dev_xp)
        sbuf[2, a, cs] = fbuf[3, a, cs].astype(BF)
        sbuf[2, b, cs] = (fbuf[3, b, cs] + r1[b, cs].astype(F32)).astype(BF)
        send(at(sbuf.at[2], i), at(r2.at[1], i), x_s.at[i, 3], x_r.at[i, 3], dev_xm)

    def middle(i):
        r0, rn, c0, cn, f = cell(i)
        arrived(at(r2.at[0], i), x_s.at[i, 2], x_r.at[i, 2], dev_xm)
        arrived(at(r2.at[1], i), x_s.at[i, 3], x_r.at[i, 3], dev_xp)

        def total(r, lo):
            cs = pl.ds(lo, 128)
            return fbuf[0, r, cs] + r2[0, r, cs].astype(F32) + r2[1, r, cs].astype(F32)

        def one(k, _):
            r = pl.ds(mul_of(r0 + k * 32, 32), 32)
            if f < 3:
                gate, up = total(r, c0), total(r, c0 + 128)
                cot = hg[r, 128 * f:128 * f + 128].astype(F32)
            else:
                gate = total(r, c0)
                up = pltpu.roll(gate, 64, 1)
                cot = hgm[r, :]
            sig = jax.nn.sigmoid(gate)
            act = gate * sig
            hidden = (act * up).astype(BF)
            du = cot * act
            dg = cot * up * sig * (1.0 + gate * (1.0 - sig))
            if f < 3:
                hid[r, 128 * f:128 * f + 128] = hidden
                dbuf[x, r, c0:c0 + 128] = dg.astype(BF)
                dbuf[x, r, c0 + 128:c0 + 256] = du.astype(BF)
            else:
                hid[r, 384:448] = hidden[:, 0:64]
                dbuf[x, r, c0:c0 + 128] = jnp.where(lane[0:32] < 64, dg, pltpu.roll(du, 64, 1)).astype(BF)
            return 0

        lax.fori_loop(0, rn // 32, one, 0)
        send(at(dbuf.at[x], i), at(dbuf.at[x], i), x_s.at[i, 4], x_r.at[i, 4], dev_xp)
        send(at(dbuf.at[x], i), at(dbuf.at[x], i), x_s.at[i, 5], x_r.at[i, 5], dev_xm)

    def spread(i):
        arrived(at(dbuf.at[xm], i), x_s.at[i, 4], x_r.at[i, 4], dev_xm)
        b = at(dbuf.at[xm], i, 0.0, 0.5)
        send(b, b, x_s.at[i, 6], x_r.at[i, 6], dev_xp)
        arrived(at(dbuf.at[xp], i), x_s.at[i, 5], x_r.at[i, 5], dev_xp)
        b = at(dbuf.at[xp], i, 0.5, 1.0)
        send(b, b, x_s.at[i, 7], x_r.at[i, 7], dev_xm)

    def gathered(i):
        arrived(at(dbuf.at[x2], i, 0.0, 0.5), x_s.at[i, 6], x_r.at[i, 6], dev_xm)
        arrived(at(dbuf.at[x2], i, 0.5, 1.0), x_s.at[i, 7], x_r.at[i, 7], dev_xp)

    def bend(f):
        c0, cn = COLS[f]

        def part(row):
            acc = None
            for j in range(4):
                d = coef[j][1] * jnp.dot(xt[j, pl.ds(row, 256), :], dbuf[j, :, c0:c0 + cn],
                                         preferred_element_type=F32)
                acc = d if acc is None else acc + d
            return acc

        def one(k, _):
            q = rem(k, 2)
            mine = part(mul_of(rem(1 - g + div(k, 2), 2) * 512 + q * 256, 256))
            r = pl.ds(mul_of(q * 256, 256), 256)

            @pl.when(k < 2)
            def _():
                ysend[r, c0:c0 + cn] = mine.astype(BF)

            @pl.when(k >= 2)
            def _():
                dwown[r, c0:c0 + cn] = mine
            return 0

        lax.fori_loop(0, 4, one, 0)
        s = (slice(None), pl.ds(c0, cn))
        send(ysend.at[s], yrecv.at[s], y_s.at[f], y_r.at[f], dev_y)

    def bend_out(f):
        c0, cn = COLS[f]
        arrived(yrecv.at[:, pl.ds(c0, cn)], y_s.at[f], y_r.at[f], dev_y)

        def one(k, _):
            r = pl.ds(mul_of(k * 64, 64), 64)
            v = dwown[r, c0:c0 + cn] + yrecv[r, c0:c0 + cn].astype(F32)
            if f < 3:
                gg[r, 128 * f:128 * f + 128] = v[:, 0:128]
                ug[r, 128 * f:128 * f + 128] = v[:, 128:256]
            else:
                gg[r, 384:448] = v[:, 0:64]
                ug[r, 384:448] = pltpu.roll(v, 64, 1)[:, 0:64]
            return 0

        lax.fori_loop(0, 8, one, 0)

    def back(h):
        r0, rn = ROWS[h]

        def one(i, _):
            piece, q = rem(i, 2), div(i, 2)
            k = rem(4 + div(q + 1, 2) * (1 - 2 * rem(q, 2)) + 8, 8)
            zd, yd = rem(z + k, 8), rem(yh + piece, 2)
            jr = yd * 2 + div(zd, 4)
            v = lax.dot_general(
                dbuf[jr, r0:r0 + rn, :], wbuf[jr, pl.ds(mul_of(256 * rem(zd, 4), 256), 256), :],
                (((1,), (1,)), ((), ())), preferred_element_type=F32)
            s = piece * 8 + k
            dxo[s, r0:r0 + rn, :] = jnp.where(c == 0, v[:, 0:128], v[:, 128:256])
            dxs[s, r0:r0 + rn, :] = jnp.where(c == 0, v[:, 128:256], v[:, 0:128]).astype(BF)
            rc(dxs.at[s, pl.ds(r0, rn), :], dxr.at[s, pl.ds(r0, rn), :], dd_s.at[h, s], dd_r.at[h, s], dev_c).start()
            return 0

        lax.fori_loop(0, 16, one, 0)

    def core_sum(h, piece, k):
        r0, rn = ROWS[h]
        s = piece * 8 + k
        arrived(dxr.at[s, pl.ds(r0, rn), :], dd_s.at[h, s], dd_r.at[h, s], dev_c)
        return dxo[s, r0:r0 + rn, :] + dxr[s, r0:r0 + rn, :].astype(F32)

    def zslot(direction, piece, s):
        return (direction * 2 + piece) * 4 + s

    def back_step(h, s):
        r0, rn = ROWS[h]
        for piece in (0, 1):
            for direction in (0, 1):
                first = 4 - HOPS[direction][piece]
                if s < first:
                    continue
                k = 4 - s if direction == 0 else (8 - (4 - s)) % 8
                v = core_sum(h, piece, k)
                if s > first:
                    i = zslot(direction, piece, s - 1)
                    arrived(zr.at[i, pl.ds(r0, rn), :], dz_s.at[h, i], dz_r.at[h, i], dev_z[1 - direction])
                    v = v + zr[i, r0:r0 + rn, :].astype(F32)
                i = zslot(direction, piece, s)
                zs[i, r0:r0 + rn, :] = v.astype(BF)
                send(zs.at[i, pl.ds(r0, rn), :], zr.at[i, pl.ds(r0, rn), :], dz_s.at[h, i], dz_r.at[h, i],
                     dev_z[direction])

    def back_last(h):
        r0, rn = ROWS[h]
        rows = pl.ds(r0, rn)
        for piece in (0, 1):
            v = core_sum(h, piece, 0)
            for direction in (0, 1):
                i = zslot(direction, piece, 3)
                arrived(zr.at[i, rows, :], dz_s.at[h, i], dz_r.at[h, i], dev_z[1 - direction])
                v = v + zr[i, r0:r0 + rn, :].astype(F32)
            fs[piece, r0:r0 + rn, :] = v.astype(BF)
            if piece == 0:
                @pl.when(away)
                def _():
                    rc(fs.at[0, rows, :], fr.at[0, rows, :], f_s.at[h, 0], f_r.at[h, 0], dev_p).start()

                @pl.when(jnp.logical_not(away))
                def _():
                    fr[0, r0:r0 + rn, :] = fs[0, r0:r0 + rn, :]
            else:
                send(fs.at[1, rows, :], fr.at[1, rows, :], f_s.at[h, 1], f_r.at[h, 1], dev_s2)

    def back_out(h):
        r0, rn = ROWS[h]
        rows = pl.ds(r0, rn)

        @pl.when(away)
        def _():
            arrived(fr.at[0, rows, :], f_s.at[h, 0], f_r.at[h, 0], dev_p)

        arrived(fr.at[1, rows, :], f_s.at[h, 1], f_r.at[h, 1], dev_d2)
        ig[r0:r0 + rn, :] = (fr[0, r0:r0 + rn, :].astype(F32) + fr[1, r0:r0 + rn, :].astype(F32)).astype(BF)

    for h in range(NH):
        tok_scatter(h)
    for f in range(3):
        w_send(f)
    pack()
    w_send(3)
    for f in range(NF):
        blend(f, True)
    for s in range(5):
        for h in range(NH):
            tok_step(h, s)
    for h in range(NH):
        tok_done(h)
        tok_transpose(h)

    blended = set()

    def ready(i):
        f = CELLS[i][1]
        if f not in blended:
            w_arrive(f)
            blend(f, False)
            blended.add(f)

    left_f = {f: sum(1 for a in CELLS if a[1] == f) for f in range(NF)}
    left_h = {h: sum(1 for a in CELLS if a[0] == h) for h in range(NH)}
    queue = []

    def finish(i):
        h, f = CELLS[i]
        gathered(i)
        left_f[f] -= 1
        left_h[h] -= 1
        if left_h[h] == 0:
            back(h)
            queue.extend([functools.partial(back_step, h, s) for s in range(4)]
                         + [functools.partial(back_last, h), functools.partial(back_out, h)])
        if left_f[f] == 0:
            if queue:
                queue.pop(0)()
            bend(f)

    def step_back(last):
        if queue and not last:
            queue.pop(0)()

    for n in range(NC + 2):
        if n < NC:
            ready(n)
            forward(n)
        if 1 <= n <= NC:
            middle(n - 1)
        step_back(n >= NC)
        if n < NC:
            reduce(n)
        if 1 <= n <= NC:
            spread(n - 1)
        step_back(n >= NC)
        if n >= 2:
            finish(n - 2)
    outs = list(range(NF))
    while queue:
        queue.pop(0)()
        if outs:
            bend_out(outs.pop(0))
    while outs:
        bend_out(outs.pop(0))

    for d in sent:
        d.wait_send()
    for h in range(NH):
        r0, rn = ROWS[h]

        @pl.when(away)
        def _():
            rc(tok.at[pl.ds(r0, rn), :], block(pq, h), p0_s.at[h, 0], p0_r.at[h, 0], dev_p).wait_send()
            rc(fs.at[0, pl.ds(r0, rn), :], fr.at[0, pl.ds(r0, rn), :], f_s.at[h, 0], f_r.at[h, 0], dev_p).wait_send()

        def drain(s, _):
            rc(dxs.at[s, pl.ds(r0, rn), :], dxr.at[s, pl.ds(r0, rn), :], dd_s.at[h, s], dd_r.at[h, s],
               dev_c).wait_send()
            return 0

        lax.fori_loop(0, 16, drain, 0)


def per_device(tokens, t_values, *rest):
    v = pl.BlockSpec(memory_space=pltpu.VMEM)
    dma = pltpu.SemaphoreType.DMA
    scratch = [
        pltpu.VMEM((2048, 1024), BF),
        pltpu.VMEM((4, 1024, 512), BF),
        pltpu.VMEM((21, 512, 128), BF),
        pltpu.VMEM((3, 512, 128), BF),
        pltpu.VMEM((4, 1024, 896), BF),
        pltpu.VMEM((4, 512, 896), F32),
        pltpu.VMEM((3, 512, 896), BF),
        pltpu.VMEM((512, 896), BF),
        pltpu.VMEM((2, 512, 896), BF),
        pltpu.VMEM((4, 512, 896), BF),
        pltpu.VMEM((512, 896), F32),
        pltpu.VMEM((512, 896), BF),
        pltpu.VMEM((512, 896), BF),
        pltpu.VMEM((16, 512, 128), F32),
        pltpu.VMEM((16, 512, 128), BF),
        pltpu.VMEM((16, 512, 128), BF),
        pltpu.VMEM((16, 512, 128), BF),
        pltpu.VMEM((16, 512, 128), BF),
        pltpu.VMEM((2, 512, 128), BF),
        pltpu.VMEM((2, 512, 128), BF),
        pltpu.VMEM((512, 128), F32),
        pltpu.VMEM((512, 128), F32),
        pltpu.VMEM((512, 128), F32),
    ]
    for shape in ((NH, 2), (NH, 2, 2, 4), (NH, 16), (21,), (NC, 8), (NF,), (NH, 16), (NH, 16), (NH, 2)):
        scratch += [dma(shape), dma(shape)]
    return tuple(
        pl.pallas_call(
            kernel,
            out_shape=(
                jax.ShapeDtypeStruct((512, 448), BF),
                jax.ShapeDtypeStruct((512, 128), BF),
                jax.ShapeDtypeStruct((512, 448), F32),
                jax.ShapeDtypeStruct((512, 448), F32),
            ),
            in_specs=[v, pl.BlockSpec(memory_space=pltpu.SMEM)] + [v] * 7,
            out_specs=(v, v, v, v),
            scratch_shapes=scratch,
            compiler_params=pltpu.CompilerParams(
                collective_id=0, has_side_effects=True, vmem_limit_bytes=66_000_000
            ),
        )(tokens, t_values, *rest)
    )


def solution(mesh):
    return jax.shard_map(
        per_device,
        mesh=mesh,
        in_specs=(P("pt", "tp"), P()) + (P("pt", "tp"),) * 7,
        out_specs=(P("pt", "tp"),) * 4,
        check_vma=False,
    )
```

time: 383 us -> 211 us (0.55)
  the two profiles are of different devices: /device:TPU:3 before, /device:TPU:34 now
where the time goes in v1:
time: 211 us; the launch traced here: 210 us
  Pallas kernels  195 us (92%)
  local copies, waits for them, and re-layouts  14.7 us (7%)
    pallas_call x1, Pallas kernels, per_device(): pl.pallas_call(kernel, out_shape=(jax.ShapeDtypeStruct((512, 448), BF), j...  195 us
    unnamed x24, local copies, waits for them, and re-layouts  8.85 us
    pallas_call x3, local copies, waits for them, and re-layouts, per_device(): pl.pallas_call(kernel, out_shape=(jax.ShapeDtypeStruct((512, 448), BF), j...  5.8 us

profile of v1, /device:TPU:34, one launch (start us, length us, event | category | flops | bytes accessed | tf_op | source)
XLA Modules:
  0.0 210.1 jit_solution(1073407836601472411)
XLA Ops:
  0.6 0.0 copy-start.1
  0.6 2.1 copy.13.gs
  2.7 0.0 copy-done.1
  2.7 0.0 copy-start.2
  2.7 1.0 copy.14.gb
  3.7 0.0 copy-done.2
  3.7 0.0 copy-start.3
  3.7 1.0 copy.15.ge
  4.8 0.0 copy-done.3
  4.8 0.0 copy-start.4
  4.8 1.0 copy.16.us
  5.8 0.0 copy-done.4
  5.8 0.0 copy-start.5
  5.8 1.0 copy.17.ub
  6.8 0.0 copy-done.5
  6.8 0.0 copy-start.6
  6.8 1.0 copy.18.ue
  7.8 0.0 copy-done.6
  7.8 1.0 copy.19.hg
  8.8 194.8 %shard_map.120 = (bf16[512,448]{1,0:T(8,128)(2,1)}, bf16[512,128]{1,0:T(8,128)(2,1)}, f32[512,448]{1,0:T(8,128)}, f32[512,448]{1,0:T(8,128)}) custom-call(bf16[512,128]{1,0:T(8,128)(2,1)} %tok.1, f32[8]{0:T(128)} %ts.1, bf16[512,448]{1,0:T(8,128)(2,1)} %copy.13.gs, bf16[512,448]{1,0:T(8,128)(2,1)} %copy.14.gb, bf16[512,448]{1,0:T(8,128)(2,1)} %copy.15.ge, ...), custom_call_target="tpu_custom_call" | custom-call | tf_op jit(solution)/shard_map/pallas_call | solution.py:539
  203.7 2.0 copy.20
  205.7 0.0 copy-start
  205.7 2.6 %copy.21 = f32[512,448]{0,1:T(8,128)} copy(f32[512,448]{1,0:T(8,128)} %get-tuple-element.6) | data formatting | bytes 1835008 | tf_op jit(solution)/shard_map/pallas_call | solution.py:539
  208.2 0.0 copy-done
  208.2 0.0 copy-start.7
  208.2 1.2 copy.22
  209.5 0.0 copy-done.7
  209.5 0.7 copy.24
Async XLA Ops:
  0.6 2.1 copy-start.1
  2.7 1.0 copy-start.2
  3.7 1.0 copy-start.3
  4.8 1.0 copy-start.4
  5.8 1.0 copy-start.5
  6.8 1.0 copy-start.6
  205.7 2.6 %copy-start = (f32[512,448]{1,0:T(8,128)S(1)}, f32[512,448]{1,0:T(8,128)}, u32[]{:S(2)}) copy-start(f32[512,448]{1,0:T(8,128)} %get-tuple-element.7) | copy-start | bytes 2752516
  208.2 1.2 copy-start.7

commit v2 on v0

v2 whole, which is shorter than its diff:
```python
import jax
import jax.numpy as jnp
from jax import lax
from jax.experimental import pallas as pl
from jax.experimental.pallas import tpu as pltpu
from jax.sharding import PartitionSpec as P

MESH = pl.DeviceIdType.MESH
F32, BF = jnp.float32, jnp.bfloat16

TOKS = ((0, 256), (256, 256))
UNITS = ((0, 256), (256, 256), (512, 256), (768, 128))
CELLS = ((0, 0), (1, 0), (0, 1), (1, 1), (0, 2), (0, 3), (1, 2), (1, 3))
NH, NF, NC = len(TOKS), len(UNITS), len(CELLS)
HOPS = ((4, 3), (3, 4))


def div(a, b):
    return lax.div(a, jnp.int32(b))


def rem(a, b):
    return lax.rem(a, jnp.int32(b))


def mul_of(a, b):
    return pl.multiple_of(a, b)


def kernel(
    tok_in, ts_in, gs, gb, ge, us, ub, ue, hg_in,
    hid_out, ig_out, gg_out, ug_out,
    ts, tok, tokt, raw, rawp, hg, hid, ig, xt, xb, wbuf, fbuf, sbuf, r1, r2, dbuf, dn, dw, ysend, yrecv,
    dxo, dxs, dxr, zs, zr, fs, fr,
    l_s, o_s,
    p0_s, p0_r, tz_s, tz_r, td_s, td_r, w_s, w_r, x_s, x_r, y_s, y_r,
    dd_s, dd_r, dz_s, dz_r, f_s, f_r,
):
    p, t = lax.axis_index("pt"), lax.axis_index("tp")
    x, g = div(p, 2), rem(p, 2)
    yh, z, c = div(t, 16), rem(div(t, 2), 8), rem(t, 2)
    xp, xm, x2 = rem(x + 1, 4), rem(x + 3, 4), rem(x + 2, 4)
    dev_xp, dev_xm = (2 * xp + g, t), (2 * xm + g, t)
    dev_y = (2 * x + (1 - g), t)
    dev_c = (p, yh * 16 + z * 2 + (1 - c))
    dev_z = ((p, yh * 16 + rem(z + 1, 8) * 2 + c), (p, yh * 16 + rem(z + 7, 8) * 2 + c))
    mirror = div(z, 4) != rem(x, 2)
    zq = jnp.where(mirror, 7 - z, z)
    pp, pq = 2 * div(t, 8) + g, div(x, 2) * 16 + zq * 2 + c
    t2 = rem(t + 16, 32)
    dev_p = (pp, pq)
    dev_d2 = (pp, rem(pq + 16, 32))
    dev_s2 = (2 * div(t2, 8) + g, pq)
    away = div(t, 8) != x

    def column(z0):
        return jnp.where(div(z0, 4) != rem(x, 2), 3 - rem(z0, 4), rem(z0, 4))

    mats = ((gs, us), (gb, ub), (ge, ue))

    def units(f):
        c0, cn = UNITS[f]
        return c0, cn, c0 // 2, cn // 2

    tok_load = pltpu.make_async_copy(tok_in, tok, l_s.at[0])
    hg_load = pltpu.make_async_copy(hg_in, hg, l_s.at[1])
    ts_load = pltpu.make_async_copy(ts_in, ts, l_s.at[2])
    tok_load.start()
    for f in range(NF):
        c0, _, u0, un = units(f)
        for m in range(3):
            for k in range(2):
                pltpu.make_async_copy(
                    mats[m][k].at[pl.ds(u0, un), :], raw.at[m, pl.ds(c0 + k * un, un), :], l_s.at[3 + f]).start()
    ts_load.start()
    hg_load.start()

    barrier = pltpu.get_barrier_semaphore()
    for dev in (dev_xp, dev_xm, dev_y, dev_c, dev_z[0], dev_z[1], dev_d2, dev_s2):
        pl.semaphore_signal(barrier, inc=1, device_id=dev, device_id_type=MESH)

    @pl.when(away)
    def _():
        pl.semaphore_signal(barrier, inc=1, device_id=dev_p, device_id_type=MESH)

    tok_load.wait()
    tokt[...] = tok[...].T
    pl.semaphore_wait(barrier, 8 + away.astype(jnp.int32))

    def rc(src, dst, ss, rs, dev):
        return pltpu.make_async_remote_copy(
            src_ref=src, dst_ref=dst, send_sem=ss, recv_sem=rs, device_id=dev, device_id_type=MESH
        )

    def send(src, dst, ss, rs, dev):
        rc(src, dst, ss, rs, dev).start()

    def arrived(dst, ss, rs, dev):
        rc(dst, dst, ss, rs, dev).wait_recv()

    def left(src, ss, rs, dev):
        rc(src, src, ss, rs, dev).wait_send()

    def block(tidx, h):
        r0, rn = TOKS[h]
        return xt.at[tidx[0], pl.ds(mul_of(128 * tidx[1], 128), 128), pl.ds(r0, rn)]

    def tblock(z0, piece, cc, h):
        return block((rem(yh + piece, 2) * 2 + div(z0, 4), column(z0) * 2 + cc), h)

    there = (x, rem(t, 8))

    def tok_scatter(h):
        r0, rn = TOKS[h]
        mine = tokt.at[:, pl.ds(r0, rn)]

        @pl.when(away)
        def _():
            send(mine, block(there, h), p0_s.at[0], p0_r.at[h, 0], dev_p)

        send(mine, block(there, h), p0_s.at[1], p0_r.at[h, 1], dev_d2)

        @pl.when(jnp.logical_not(away))
        def _():
            block(there, h)[...] = tokt[:, pl.ds(r0, rn)]

    def tok_arrive(h, piece):
        b = tblock(z, piece, c, h)
        if piece == 0:
            @pl.when(away)
            def _():
                arrived(b, p0_s.at[0], p0_r.at[h, 0], dev_p)
        else:
            arrived(b, p0_s.at[1], p0_r.at[h, 1], dev_d2)

    def z_at(direction, s):
        return rem(z + 8 - s, 8) if direction == 0 else rem(z + s, 8)

    def ring_wait(h, s, piece):
        r0, rn = TOKS[h]
        n = sum(s < HOPS[d][piece] for d in (0, 1))
        arrived(zr.at[pl.ds(0, n), pl.ds(0, rn), :], tz_s.at[h], tz_r.at[h, s, piece], dev_z[0])

    def tok_step(h, s):
        for piece in (0, 1):
            if s == 0:
                tok_arrive(h, piece)
            elif s <= max(HOPS[0][piece], HOPS[1][piece]):
                ring_wait(h, s - 1, piece)
            for direction in (0, 1):
                if s < HOPS[direction][piece]:
                    b = tblock(z_at(direction, s), piece, c, h)
                    send(b, b, tz_s.at[h], tz_r.at[h, s, piece], dev_z[direction])
            for direction in (0, 1):
                if s <= HOPS[direction][piece] and (s > 0 or direction == 0):
                    b = tblock(z_at(direction, s), piece, c, h)
                    send(b, b, td_s.at[h], td_r.at[h], dev_c)

    def tok_done(h):
        r0, rn = TOKS[h]
        arrived(xt.at[:, pl.ds(0, 512), pl.ds(r0, rn)], td_s.at[h], td_r.at[h], dev_c)

    def tok_turn(h):
        r0, rn = TOKS[h]

        def one(i, _):
            jr, cb = div(i, 8), rem(i, 8)
            d = pl.ds(mul_of(128 * cb, 128), 128)
            xb[jr, r0:r0 + rn, d] = xt[jr, d, r0:r0 + rn].T
            return 0

        lax.fori_loop(0, 32, one, 0)

    def w_send(f):
        c0, cn = UNITS[f]
        b = raw.at[:, pl.ds(c0, cn), :]
        pltpu.make_async_copy(b, b, l_s.at[3 + f]).wait()
        send(b, rawp.at[:, pl.ds(c0, cn), :], w_s.at[0], w_r.at[f], dev_y)

    def w_arrive(f):
        c0, cn = UNITS[f]
        arrived(rawp.at[:, pl.ds(c0, cn), :], w_s.at[0], w_r.at[f], dev_y)

    ts_load.wait()
    tv = [ts[2 * j + g] for j in range(4)]
    coef = [((1.0 - v) * (1.0 - v), 2.0 * v * (1.0 - v), v * v) for v in tv]

    def blend(f, own):
        c0, cn = UNITS[f]
        src, side = (raw, g) if own else (rawp, 1 - g)
        lanes = pl.ds(mul_of(side * 512, 512), 512)

        def one(i, _):
            r = pl.ds(mul_of(c0 + i * 16, 16), 16)
            v = [src[m, r, :].astype(F32) for m in range(3)]
            for j in range(4):
                b0, b1, b2 = coef[j]
                wbuf[j, r, lanes] = (b0 * v[0] + b1 * v[1] + b2 * v[2]).astype(BF)
            return 0

        lax.fori_loop(0, cn // 16, one, 0)

    def cell(i):
        h, f = CELLS[i]
        return TOKS[h] + UNITS[f] + (f,)

    def at(ref, i, half=None):
        r0, rn, c0, cn, _ = cell(i)
        if half is not None:
            c0, cn = c0 + half * (cn // 2), cn // 2
        return ref.at[pl.ds(c0, cn), pl.ds(r0, rn)]

    def forward(i):
        r0, rn, c0, cn, _ = cell(i)

        def one(k, _):
            for q in (2 * k, 2 * k + 1):
                jr = rem(x + q, 4)
                fbuf[q, c0:c0 + cn, r0:r0 + rn] = jnp.dot(
                    wbuf[jr, c0:c0 + cn, :], xt[jr, :, r0:r0 + rn], preferred_element_type=F32)
            return 0

        lax.fori_loop(0, 2, one, 0)
        sbuf[0, c0:c0 + cn, r0:r0 + rn] = fbuf[2, c0:c0 + cn, r0:r0 + rn].astype(BF)
        send(at(sbuf.at[0], i, 0), at(r1, i, 0), x_s.at[0], x_r.at[i, 0], dev_xp)
        send(at(sbuf.at[0], i, 1), at(r1, i, 1), x_s.at[0], x_r.at[i, 0], dev_xm)

    def reduce(i):
        r0, rn, c0, cn, _ = cell(i)
        n = cn // 2
        a, b, cs = slice(c0, c0 + n), slice(c0 + n, c0 + cn), slice(r0, r0 + rn)
        arrived(at(r1, i), x_s.at[0], x_r.at[i, 0], dev_xm)
        sbuf[1, a, cs] = (fbuf[1, a, cs] + r1[a, cs].astype(F32)).astype(BF)
        sbuf[1, b, cs] = fbuf[1, b, cs].astype(BF)
        send(at(sbuf.at[1], i), at(r2.at[0], i), x_s.at[0], x_r.at[i, 1], dev_xp)
        sbuf[2, a, cs] = fbuf[3, a, cs].astype(BF)
        sbuf[2, b, cs] = (fbuf[3, b, cs] + r1[b, cs].astype(F32)).astype(BF)
        send(at(sbuf.at[2], i), at(r2.at[1], i), x_s.at[0], x_r.at[i, 1], dev_xm)

    def two(i):
        r0, rn, c0, cn, _ = cell(i)
        return r2.at[:, pl.ds(c0, cn), pl.ds(r0, rn)]

    def middle(i):
        r0, rn, c0, cn, f = cell(i)
        arrived(two(i), x_s.at[0], x_r.at[i, 1], dev_xm)
        cs = slice(r0, r0 + rn)

        def total(r):
            return fbuf[0, r, cs] + r2[0, r, cs].astype(F32) + r2[1, r, cs].astype(F32)

        def one(k, _):
            rg = pl.ds(mul_of(c0 + k * 16, 16), 16)
            ru = pl.ds(mul_of(c0 + cn // 2 + k * 16, 16), 16)
            rh = pl.ds(mul_of(c0 // 2 + k * 16, 16), 16)
            gate, up = total(rg), total(ru)
            cot = hg[rh, cs].astype(F32)
            sig = jax.nn.sigmoid(gate)
            act = gate * sig
            hid[rh, cs] = (act * up).astype(BF)
            dbuf[x, rg, cs] = (cot * up * sig * (1.0 + gate * (1.0 - sig))).astype(BF)
            dbuf[x, ru, cs] = (cot * act).astype(BF)
            return 0

        lax.fori_loop(0, cn // 32, one, 0)
        send(at(dbuf.at[x], i), at(dbuf.at[x], i), x_s.at[0], x_r.at[i, 2], dev_xp)
        send(at(dbuf.at[x], i), at(dbuf.at[x], i), x_s.at[0], x_r.at[i, 2], dev_xm)

    def spread(i):
        arrived(two(i), x_s.at[0], x_r.at[i, 2], dev_xm)
        b = at(dbuf.at[xm], i, 0)
        send(b, b, x_s.at[0], x_r.at[i, 3], dev_xp)
        b = at(dbuf.at[xp], i, 1)
        send(b, b, x_s.at[0], x_r.at[i, 3], dev_xm)

    def gathered(i):
        arrived(at(r1, i), x_s.at[0], x_r.at[i, 3], dev_xm)

    def turn(i):
        r0, rn, c0, cn, _ = cell(i)

        def one(j, _):
            dn[j, r0:r0 + rn, c0:c0 + cn] = dbuf[j, c0:c0 + cn, r0:r0 + rn].T
            return 0

        lax.fori_loop(0, 4, one, 0)

    def bend(f):
        c0, cn = UNITS[f]

        def part(lanes):
            acc = None
            for j in range(4):
                d = coef[j][1] * jnp.dot(dbuf[j, c0:c0 + cn, :], xb[j, :, lanes], preferred_element_type=F32)
                acc = d if acc is None else acc + d
            return acc

        def one(k, _):
            q = rem(k, 2)
            mine = part(pl.ds(mul_of(rem(1 - g + div(k, 2), 2) * 512 + q * 256, 256), 256))
            r = pl.ds(mul_of(q * 256, 256), 256)

            @pl.when(k < 2)
            def _():
                ysend[c0:c0 + cn, r] = mine.astype(BF)

            @pl.when(k >= 2)
            def _():
                dw[c0:c0 + cn, r] = mine
            return 0

        lax.fori_loop(0, 4, one, 0)
        send(ysend.at[pl.ds(c0, cn), :], yrecv.at[pl.ds(c0, cn), :], y_s.at[0], y_r.at[f], dev_y)

    def dw_out(f, k):
        c0, _, u0, un = units(f)
        return pltpu.make_async_copy(
            dw.at[pl.ds(c0 + k * un, un), :], (gg_out, ug_out)[k].at[pl.ds(u0, un), :], o_s.at[2])

    hid_copy = pltpu.make_async_copy(hid, hid_out, o_s.at[0])
    ig_copy = pltpu.make_async_copy(ig, ig_out, o_s.at[1])

    def bend_out(f):
        c0, cn = UNITS[f]
        arrived(yrecv.at[pl.ds(c0, cn), :], y_s.at[0], y_r.at[f], dev_y)

        def one(k, _):
            r = pl.ds(mul_of(c0 + k * 32, 32), 32)
            dw[r, :] = dw[r, :] + yrecv[r, :].astype(F32)
            return 0

        lax.fori_loop(0, cn // 32, one, 0)
        dw_out(f, 0).start()
        dw_out(f, 1).start()

    def back(h, part):
        r0, rn = TOKS[h]
        rows = pl.ds(r0, rn)

        def one(piece, _):
            for k in ((4,), (3, 5), (2, 6), (1, 7), (0,))[part]:
                zd, yd = rem(z + k, 8), rem(yh + piece, 2)
                jr = yd * 2 + div(zd, 4)
                v = jnp.dot(dn[jr, r0:r0 + rn, :], wbuf[jr, :, pl.ds(mul_of(256 * column(zd), 256), 256)],
                            preferred_element_type=F32)
                s = k * 2 + piece
                dxo[s, r0:r0 + rn, :] = jnp.where(c == 0, v[:, 0:128], v[:, 128:256])
                dxs[s, r0:r0 + rn, :] = jnp.where(c == 0, v[:, 128:256], v[:, 0:128]).astype(BF)
                send(dxs.at[s, rows, :], dxr.at[s, rows, :], dd_s.at[h], dd_r.at[h, part], dev_c)
            return 0

        lax.fori_loop(0, 2, one, 0)

    def core_sum(h, piece, k):
        r0, rn = TOKS[h]
        s = k * 2 + piece
        return dxo[s, r0:r0 + rn, :] + dxr[s, r0:r0 + rn, :].astype(F32)

    def core_wait(h, part):
        r0, rn = TOKS[h]
        n = 2 if part in (0, 4) else 4
        arrived(dxr.at[pl.ds(0, n), pl.ds(r0, rn), :], dd_s.at[h], dd_r.at[h, part], dev_c)

    def zslot(direction, piece, s):
        return (direction * 2 + piece) * 4 + s

    def back_wait(h, s, piece):
        r0, rn = TOKS[h]
        n = sum(s >= 4 - HOPS[d][piece] for d in (0, 1))
        arrived(zr.at[pl.ds(0, n), pl.ds(r0, rn), :], dz_s.at[h], dz_r.at[h, s, piece], dev_z[0])

    def back_step(h, s):
        r0, rn = TOKS[h]
        core_wait(h, s)
        for piece in (0, 1):
            if s > 4 - max(HOPS[0][piece], HOPS[1][piece]):
                back_wait(h, s - 1, piece)
            for direction in (0, 1):
                first = 4 - HOPS[direction][piece]
                if s < first:
                    continue
                k = 4 - s if direction == 0 else 4 + s
                v = core_sum(h, piece, k)
                if s > first:
                    v = v + zr[zslot(direction, piece, s - 1), r0:r0 + rn, :].astype(F32)
                i = zslot(direction, piece, s)
                zs[i, r0:r0 + rn, :] = v.astype(BF)
                send(zs.at[i, pl.ds(r0, rn), :], zr.at[i, pl.ds(r0, rn), :], dz_s.at[h], dz_r.at[h, s, piece],
                     dev_z[direction])

    def back_last(h):
        r0, rn = TOKS[h]
        rows = pl.ds(r0, rn)
        core_wait(h, 4)
        for piece in (0, 1):
            back_wait(h, 3, piece)
            v = core_sum(h, piece, 0)
            for direction in (0, 1):
                v = v + zr[zslot(direction, piece, 3), r0:r0 + rn, :].astype(F32)
            fs[piece, r0:r0 + rn, :] = v.astype(BF)
            if piece == 0:
                @pl.when(away)
                def _():
                    send(fs.at[0, rows, :], fr.at[0, rows, :], f_s.at[0], f_r.at[h, 0], dev_p)

                @pl.when(jnp.logical_not(away))
                def _():
                    fr[0, r0:r0 + rn, :] = fs[0, r0:r0 + rn, :]
            else:
                send(fs.at[1, rows, :], fr.at[1, rows, :], f_s.at[1], f_r.at[h, 1], dev_s2)

    def back_out(h):
        r0, rn = TOKS[h]
        rows = pl.ds(r0, rn)

        @pl.when(away)
        def _():
            arrived(fr.at[0, rows, :], f_s.at[0], f_r.at[h, 0], dev_p)

        arrived(fr.at[1, rows, :], f_s.at[1], f_r.at[h, 1], dev_d2)
        ig[r0:r0 + rn, :] = (fr[0, r0:r0 + rn, :].astype(F32) + fr[1, r0:r0 + rn, :].astype(F32)).astype(BF)

    for h in range(NH):
        tok_scatter(h)
    for f in range(NF):
        w_send(f)
    for f in range(NF):
        blend(f, True)
    hg_load.wait()
    for h, s in ((0, 0), (1, 0), (0, 1), (0, 2), (1, 1), (0, 3), (1, 2), (0, 4)):
        tok_step(h, s)
    tok_done(0)
    w_arrive(0)
    blend(0, False)
    forward(0)
    tok_step(1, 3)
    reduce(0)
    tok_step(1, 4)
    tok_done(1)
    forward(1)
    middle(0)
    reduce(1)
    spread(0)
    tok_turn(0)
    middle(1)
    gathered(0)
    turn(0)
    spread(1)
    tok_turn(1)
    w_arrive(1)
    blend(1, False)
    forward(2)
    forward(3)
    reduce(2)
    gathered(1)
    turn(1)
    reduce(3)
    middle(2)
    bend(0)
    spread(2)
    middle(3)
    w_arrive(2)
    blend(2, False)
    forward(4)
    w_arrive(3)
    blend(3, False)
    forward(5)
    spread(3)
    reduce(4)
    forward(6)
    gathered(2)
    turn(2)
    reduce(5)
    middle(4)
    forward(7)
    gathered(3)
    turn(3)
    spread(4)
    reduce(6)
    middle(5)
    bend(1)
    reduce(7)
    spread(5)
    middle(6)
    bend_out(0)
    gathered(4)
    turn(4)
    middle(7)
    hid_copy.start()
    gathered(5)
    turn(5)
    spread(6)
    back(0, 0)
    back_step(0, 0)
    back(0, 1)
    spread(7)
    back_step(0, 1)
    back(0, 2)
    back_step(0, 2)
    gathered(6)
    turn(6)
    back(0, 3)
    gathered(7)
    turn(7)
    back(1, 0)
    back_step(0, 3)
    back_step(1, 0)
    back(1, 1)
    back(0, 4)
    back_step(1, 1)
    back_last(0)
    back(1, 2)
    bend(2)
    back_step(1, 2)
    back(1, 3)
    bend(3)
    back_step(1, 3)
    back(1, 4)
    bend_out(1)
    back_out(0)
    back_last(1)
    bend_out(2)
    bend_out(3)
    back_out(1)
    ig_copy.start()

    hid_copy.wait()
    pltpu.make_async_copy(dw, dw, o_s.at[2]).wait()

    @pl.when(away)
    def _():
        left(tokt, p0_s.at[0], p0_r.at[0, 0], dev_p)
        left(fs.at[0], f_s.at[0], f_r.at[0, 0], dev_p)

    left(tokt, p0_s.at[1], p0_r.at[0, 1], dev_d2)
    left(fs.at[1], f_s.at[1], f_r.at[0, 1], dev_s2)
    left(raw, w_s.at[0], w_r.at[0], dev_y)
    left(ysend, y_s.at[0], y_r.at[0], dev_y)
    left(fbuf.at[pl.ds(0, 3)], x_s.at[0], x_r.at[0, 0], dev_xp)
    for h in range(NH):
        r0, rn = TOKS[h]
        rows = pl.ds(r0, rn)
        left(zs.at[pl.ds(0, 14), rows, :], tz_s.at[h], tz_r.at[h, 0, 0], dev_z[0])
        left(zs.at[pl.ds(0, 14), rows, :], dz_s.at[h], dz_r.at[h, 0, 0], dev_z[0])
        left(dxs.at[:, rows, :], td_s.at[h], td_r.at[h], dev_c)
        left(dxs.at[:, rows, :], dd_s.at[h], dd_r.at[h, 0], dev_c)
    ig_copy.wait()


def hand_on(*refs):
    srcs, dsts, held = refs[0:4], refs[4:8], refs[8:12]
    s_in, s_out = refs[12], refs[13]
    ins = [pltpu.make_async_copy(srcs[i], held[i], s_in.at[i]) for i in range(4)]
    outs = [pltpu.make_async_copy(held[i], dsts[i], s_out.at[i]) for i in range(4)]
    for i in range(4):
        ins[i].start()
    for i in range(4):
        ins[i].wait()
        outs[i].start()
    for i in range(4):
        outs[i].wait()


def per_device(tokens, t_values, *rest):
    a = pl.BlockSpec(memory_space=pl.ANY)
    dma = pltpu.SemaphoreType.DMA
    vm = pltpu.VMEM
    scratch = [
        pltpu.SMEM((8,), F32),
        vm((512, 128), BF),
        vm((128, 512), BF),
        vm((3, 896, 512), BF),
        vm((3, 896, 512), BF),
        vm((448, 512), BF),
        vm((448, 512), BF),
        vm((512, 128), BF),
        vm((4, 1024, 512), BF),
        vm((4, 512, 1024), BF),
        vm((4, 896, 1024), BF),
        vm((4, 896, 512), F32),
        vm((3, 896, 512), BF),
        vm((896, 512), BF),
        vm((2, 896, 512), BF),
        vm((4, 896, 512), BF),
        vm((4, 512, 896), BF),
        vm((896, 512), F32),
        vm((896, 512), BF),
        vm((896, 512), BF),
        vm((16, 512, 128), F32),
        vm((16, 512, 128), BF),
        vm((16, 512, 128), BF),
        vm((16, 512, 128), BF),
        vm((16, 512, 128), BF),
        vm((2, 512, 128), BF),
        vm((2, 512, 128), BF),
        dma((3 + NF,)),
        dma((3,)),
    ]
    for out, into in (((2,), (NH, 2)), ((NH,), (NH, 4, 2)), ((NH,), (NH,)), ((1,), (NF,)), ((1,), (NC, 4)),
                      ((1,), (NF,)), ((NH,), (NH, 5)), ((NH,), (NH, 4, 2)), ((2,), (NH, 2))):
        scratch += [dma(out), dma(into)]
    shapes = (
        jax.ShapeDtypeStruct((448, 512), BF),
        jax.ShapeDtypeStruct((512, 128), BF),
        jax.ShapeDtypeStruct((448, 512), F32),
        jax.ShapeDtypeStruct((448, 512), F32),
    )
    results = pl.pallas_call(
        kernel,
        out_shape=shapes,
        in_specs=[a] * 9,
        out_specs=(a, a, a, a),
        scratch_shapes=scratch,
        compiler_params=pltpu.CompilerParams(
            collective_id=0, has_side_effects=True, vmem_limit_bytes=67_043_328
        ),
    )(tokens, t_values, *(w.T for w in rest))
    hidden, input_grad, gate_grad, up_grad = pl.pallas_call(
        hand_on,
        out_shape=shapes,
        in_specs=[a] * 4,
        out_specs=(a, a, a, a),
        scratch_shapes=[vm(v.shape, v.dtype) for v in shapes] + [dma((4,)), dma((4,))],
    )(*results)
    return hidden.T, input_grad, gate_grad.T, up_grad.T


def solution(mesh):
    return jax.shard_map(
        per_device,
        mesh=mesh,
        in_specs=(P("pt", "tp"), P()) + (P("pt", "tp"),) * 7,
        out_specs=(P("pt", "tp"),) * 4,
        check_vma=False,
    )
```

time: 383 us -> 165 us (0.43)
  waiting for transfers between devices: 191 us -> 0 us
  Pallas kernels: 0 us -> 162 us
  blocking collectives: 101 us -> 0 us
  matrix products: 30.3 us -> 0 us
  other arithmetic: 28 us -> 0 us
  between operations: 14.1 us -> 0.64 us
  local copies, waits for them, and re-layouts: 12.9 us -> 0 us
  starting transfers between devices: 5.32 us -> 0 us
    pallas_call x0 -> x2, Pallas kernels: none -> 162 us  [the longest x1 160 us: per_device(): pl.pallas_call(kernel, out_shape=shapes, in_specs=[a] * 9, out_specs=(a,...]
    all_to_all x1 -> x0, blocking collectives: 101 us -> none  [summed_on_arrival(): lax.all_to_all(parts, axis, split_axis=0, concat_axis=0, tiled=True)]
    all_to_all x1 -> x0, waiting for transfers between devices: 96.8 us -> none  [in_one_piece(): lax.all_to_all(both, axis, split_axis=split_dim, concat_axis=concat_dim,...]
    reduce_scatter x1 -> x0, waiting for transfers between devices: 79.4 us -> none  [in_one_piece_2(): lax.psum_scatter(both, axis, scatter_dimension=dim, tiled=True)]
    dot_general x6 -> x0, matrix products: 30.3 us -> none  [the longest x1 6.75 us: per_device(): up = jnp.dot(whole, up_w, preferred_element_type=jnp.float32)]
    concatenate x2 -> x0, other arithmetic: 15.7 us -> none  [the longest x1 9.42 us: in_one_piece(): both = jnp.concatenate(arrays, axis=along)]
    all_gather x1 -> x0, waiting for transfers between devices: 13.7 us -> none  [per_device(): whole = lax.all_gather(tokens, 'tp', axis=1, tiled=True)]
    convert_element_type x6 -> x0, local copies, waits for them, and re-layouts: 10.3 us -> none  [the longest x2 3.5 us: blend_all(): end.astype(jnp.float32)[None]]
  transfers between devices with their start and end apart: 3 -> 0, of which waited for: 3 -> 0; matrix products, arithmetic and copies ran while one was open for 11% -> 0% of each run, Pallas kernels for 0% -> 0%
where the time goes in v2:
time: 165 us; the launch traced here: 163 us
  Pallas kernels  162 us (98%)
    pallas_call x1, Pallas kernels, per_device(): pl.pallas_call(kernel, out_shape=shapes, in_specs=[a] * 9, out_specs=(a,...  160 us

profile of v2, /device:TPU:3, one launch (start us, length us, event | category | flops | bytes accessed | tf_op | source)
XLA Modules:
  0.0 163.1 jit_solution(12631293128368748450)
XLA Ops:
  0.6 159.8 %shard_map.120 = (bf16[448,512]{1,0:T(8,128)(2,1)}, bf16[512,128]{1,0:T(8,128)(2,1)}, f32[448,512]{1,0:T(8,128)}, f32[448,512]{1,0:T(8,128)}) custom-call(bf16[512,128]{1,0:T(8,128)(2,1)} %tok_in.1, f32[8]{0:T(128)} %ts_in.1, bf16[448,512]{1,0:T(8,128)(2,1)} %bitcast.10, bf16[448,512]{1,0:T(8,128)(2,1)} %bitcast.11, bf16[448,512]{1,0:T(8,128)(2,1)} %bitcast.12, ...), custom_call_target="tpu_custom_call" | custom-call | tf_op jit(solution)/shard_map/pallas_call | solution.py:608
  160.4 2.7 %shard_map.121 = (bf16[448,512]{1,0:T(8,128)(2,1)}, bf16[512,128]{1,0:T(8,128)(2,1)}, f32[448,512]{1,0:T(8,128)}, f32[448,512]{1,0:T(8,128)}) custom-call(bf16[448,512]{1,0:T(8,128)(2,1)} %get-tuple-element.12.refs_0_, bf16[512,128]{1,0:T(8,128)(2,1)} %get-tuple-element.13.refs_1_, f32[448,512]{1,0:T(8,128)} %get-tuple-element.14.refs_2_, ...), custom_call_target="tpu_custom_call" | custom-call | tf_op jit(solution)/shard_map/pallas_call | solution.py:618

commit v3 on v2

--- a/solution.py
+++ b/solution.py
@@ -10,7 +10,7 @@
 
 TOKS = ((0, 256), (256, 256))
 UNITS = ((0, 256), (256, 256), (512, 256), (768, 128))
-CELLS = ((0, 0), (1, 0), (0, 1), (1, 1), (0, 2), (0, 3), (1, 2), (1, 3))
+CELLS = ((0, 0), (1, 0), (0, 1), (0, 2), (0, 3), (1, 1), (1, 2), (1, 3))
 NH, NF, NC = len(TOKS), len(UNITS), len(CELLS)
 HOPS = ((4, 3), (3, 4))
 
@@ -30,7 +30,7 @@
 def kernel(
     tok_in, ts_in, gs, gb, ge, us, ub, ue, hg_in,
     hid_out, ig_out, gg_out, ug_out,
-    ts, tok, tokt, raw, rawp, hg, hid, ig, xt, xb, wbuf, fbuf, sbuf, r1, r2, dbuf, dn, dw, ysend, yrecv,
+    ts, tok, tokt, raw, rawp, hg, hid, ig, xt, wbuf, fbuf, sbuf, r1, r2, dbuf, dn, dw, ysend, yrecv,
     dxo, dxs, dxr, zs, zr, fs, fr,
     l_s, o_s,
     p0_s, p0_r, tz_s, tz_r, td_s, td_r, w_s, w_r, x_s, x_r, y_s, y_r,
@@ -160,21 +160,14 @@
         r0, rn = TOKS[h]
         arrived(xt.at[:, pl.ds(0, 512), pl.ds(r0, rn)], td_s.at[h], td_r.at[h], dev_c)
 
-    def tok_turn(h):
-        r0, rn = TOKS[h]
-
-        def one(i, _):
-            jr, cb = div(i, 8), rem(i, 8)
-            d = pl.ds(mul_of(128 * cb, 128), 128)
-            xb[jr, r0:r0 + rn, d] = xt[jr, d, r0:r0 + rn].T
-            return 0
-
-        lax.fori_loop(0, 32, one, 0)
+    def w_here(f):
+        c0, cn = UNITS[f]
+        b = raw.at[:, pl.ds(c0, cn), :]
+        pltpu.make_async_copy(b, b, l_s.at[3 + f]).wait()
 
     def w_send(f):
         c0, cn = UNITS[f]
         b = raw.at[:, pl.ds(c0, cn), :]
-        pltpu.make_async_copy(b, b, l_s.at[3 + f]).wait()
         send(b, rawp.at[:, pl.ds(c0, cn), :], w_s.at[0], w_r.at[f], dev_y)
 
     def w_arrive(f):
@@ -291,7 +284,8 @@
         def part(lanes):
             acc = None
             for j in range(4):
-                d = coef[j][1] * jnp.dot(dbuf[j, c0:c0 + cn, :], xb[j, :, lanes], preferred_element_type=F32)
+                d = coef[j][1] * lax.dot_general(dbuf[j, c0:c0 + cn, :], xt[j, lanes, :], (((1,), (1,)), ((), ())),
+                                                 preferred_element_type=F32)
                 acc = d if acc is None else acc + d
             return acc
 
@@ -420,106 +414,118 @@
         arrived(fr.at[1, rows, :], f_s.at[1], f_r.at[h, 1], dev_d2)
         ig[r0:r0 + rn, :] = (fr[0, r0:r0 + rn, :].astype(F32) + fr[1, r0:r0 + rn, :].astype(F32)).astype(BF)
 
-    for h in range(NH):
-        tok_scatter(h)
-    for f in range(NF):
-        w_send(f)
-    for f in range(NF):
-        blend(f, True)
-    hg_load.wait()
-    for h, s in ((0, 0), (1, 0), (0, 1), (0, 2), (1, 1), (0, 3), (1, 2), (0, 4)):
-        tok_step(h, s)
+    tok_scatter(0)
+    tok_scatter(1)
+    w_here(0)
+    w_send(0)
+    w_here(1)
+    w_send(1)
+    w_here(2)
+    w_send(2)
+    w_here(3)
+    w_send(3)
+    blend(0, True)
+    blend(1, True)
+    blend(2, True)
+    blend(3, True)
+    tok_step(0, 0)
+    tok_step(1, 0)
+    tok_step(0, 1)
+    tok_step(0, 2)
+    w_arrive(0)
+    tok_step(1, 1)
+    tok_step(0, 3)
+    blend(0, False)
+    tok_step(1, 2)
+    tok_step(0, 4)
     tok_done(0)
-    w_arrive(0)
-    blend(0, False)
     forward(0)
     tok_step(1, 3)
     reduce(0)
+    w_arrive(1)
     tok_step(1, 4)
+    blend(1, False)
+    forward(2)
     tok_done(1)
+    forward(5)
     forward(1)
+    hg_load.wait()
     middle(0)
+    reduce(2)
+    reduce(5)
     reduce(1)
     spread(0)
-    tok_turn(0)
-    middle(1)
+    w_arrive(2)
+    blend(2, False)
+    forward(3)
+    forward(6)
+    middle(2)
+    reduce(3)
+    w_arrive(3)
+    blend(3, False)
+    forward(4)
+    forward(7)
+    reduce(6)
+    reduce(4)
     gathered(0)
     turn(0)
-    spread(1)
-    tok_turn(1)
-    w_arrive(1)
-    blend(1, False)
-    forward(2)
-    forward(3)
-    reduce(2)
-    gathered(1)
-    turn(1)
-    reduce(3)
-    middle(2)
-    bend(0)
+    reduce(7)
+    middle(3)
+    middle(4)
+    middle(7)
     spread(2)
-    middle(3)
-    w_arrive(2)
-    blend(2, False)
-    forward(4)
-    w_arrive(3)
-    blend(3, False)
-    forward(5)
     spread(3)
-    reduce(4)
-    forward(6)
+    spread(4)
+    middle(5)
+    middle(6)
     gathered(2)
     turn(2)
-    reduce(5)
-    middle(4)
-    forward(7)
+    middle(1)
+    hid_copy.start()
     gathered(3)
     turn(3)
-    spread(4)
-    reduce(6)
-    middle(5)
-    bend(1)
-    reduce(7)
-    spread(5)
-    middle(6)
-    bend_out(0)
     gathered(4)
     turn(4)
-    middle(7)
-    hid_copy.start()
+    spread(7)
+    back(0, 0)
+    back(0, 1)
+    back_step(0, 0)
+    back(0, 2)
+    back(0, 4)
+    spread(5)
+    back_step(0, 1)
+    spread(6)
+    spread(1)
+    back(0, 3)
     gathered(5)
     turn(5)
-    spread(6)
-    back(0, 0)
-    back_step(0, 0)
-    back(0, 1)
-    spread(7)
-    back_step(0, 1)
-    back(0, 2)
+    gathered(7)
+    turn(7)
     back_step(0, 2)
     gathered(6)
     turn(6)
-    back(0, 3)
-    gathered(7)
-    turn(7)
+    gathered(1)
+    turn(1)
     back(1, 0)
+    back_step(1, 0)
+    bend(2)
+    back(1, 1)
     back_step(0, 3)
-    back_step(1, 0)
-    back(1, 1)
-    back(0, 4)
     back_step(1, 1)
+    bend(0)
+    back(1, 2)
     back_last(0)
-    back(1, 2)
-    bend(2)
     back_step(1, 2)
+    bend(1)
     back(1, 3)
+    back_step(1, 3)
     bend(3)
-    back_step(1, 3)
     back(1, 4)
-    bend_out(1)
-    back_out(0)
     back_last(1)
     bend_out(2)
+    bend_out(0)
+    back_out(0)
+    bend_out(1)
     bend_out(3)
     back_out(1)
     ig_copy.start()
@@ -575,7 +581,6 @@
         vm((448, 512), BF),
         vm((512, 128), BF),
         vm((4, 1024, 512), BF),
-        vm((4, 512, 1024), BF),
         vm((4, 896, 1024), BF),
         vm((4, 896, 512), F32),
         vm((3, 896, 512), BF),

time: 165 us -> 147 us (0.89); the launches traced: 163 us -> 147 us
  Pallas kernels: 162 us -> 147 us
    pallas_call x1, Pallas kernels: 160 us -> 144 us  [per_device(): pl.pallas_call(kernel, out_shape=shapes, in_specs=[a] * 9, out_specs=(a,...]
where the time goes in v3:
time: 147 us
  Pallas kernels  147 us (100%)
    pallas_call x1, Pallas kernels, per_device(): pl.pallas_call(kernel, out_shape=shapes, in_specs=[a] * 9, out_specs=(a,...  144 us

profile of v3, /device:TPU:3, one launch (start us, length us, event | category | flops | bytes accessed | tf_op | source)
XLA Modules:
  0.0 147.2 jit_solution(16249879577989144689)
XLA Ops:
  0.6 143.8 %shard_map.120 = (bf16[448,512]{1,0:T(8,128)(2,1)}, bf16[512,128]{1,0:T(8,128)(2,1)}, f32[448,512]{1,0:T(8,128)}, f32[448,512]{1,0:T(8,128)}) custom-call(bf16[512,128]{1,0:T(8,128)(2,1)} %tok_in.1, f32[8]{0:T(128)} %ts_in.1, bf16[448,512]{1,0:T(8,128)(2,1)} %bitcast.10, bf16[448,512]{1,0:T(8,128)(2,1)} %bitcast.11, bf16[448,512]{1,0:T(8,128)(2,1)} %bitcast.12, ...), custom_call_target="tpu_custom_call" | custom-call | tf_op jit(solution)/shard_map/pallas_call | solution.py:613
  144.5 2.7 %shard_map.121 = (bf16[448,512]{1,0:T(8,128)(2,1)}, bf16[512,128]{1,0:T(8,128)(2,1)}, f32[448,512]{1,0:T(8,128)}, f32[448,512]{1,0:T(8,128)}) custom-call(bf16[448,512]{1,0:T(8,128)(2,1)} %get-tuple-element.12.refs_0_, bf16[512,128]{1,0:T(8,128)(2,1)} %get-tuple-element.13.refs_1_, f32[448,512]{1,0:T(8,128)} %get-tuple-element.14.refs_2_, ...), custom_call_target="tpu_custom_call" | custom-call | tf_op jit(solution)/shard_map/pallas_call | solution.py:623

commit v4 on v3

--- a/solution.py
+++ b/solution.py
@@ -518,9 +518,9 @@
     back_step(1, 2)
     bend(1)
     back(1, 3)
-    back_step(1, 3)
     bend(3)
     back(1, 4)
+    back_step(1, 3)
     back_last(1)
     bend_out(2)
     bend_out(0)

time: 147 us -> 149 us (1.014)
    pallas_call x1, Pallas kernels: 144 us -> 145 us  [per_device(): pl.pallas_call(kernel, out_shape=shapes, in_specs=[a] * 9, out_specs=(a,...]
where the time goes in v4:
time: 149 us
  Pallas kernels  148 us (99%)
    pallas_call x1, Pallas kernels, per_device(): pl.pallas_call(kernel, out_shape=shapes, in_specs=[a] * 9, out_specs=(a,...  145 us

profile of v4, /device:TPU:3, one launch (start us, length us, event | category | flops | bytes accessed | tf_op | source)
XLA Modules:
  0.0 148.8 jit_solution(2419205222027595028)
XLA Ops:
  0.6 145.5 %shard_map.120 = (bf16[448,512]{1,0:T(8,128)(2,1)}, bf16[512,128]{1,0:T(8,128)(2,1)}, f32[448,512]{1,0:T(8,128)}, f32[448,512]{1,0:T(8,128)}) custom-call(bf16[512,128]{1,0:T(8,128)(2,1)} %tok_in.1, f32[8]{0:T(128)} %ts_in.1, bf16[448,512]{1,0:T(8,128)(2,1)} %bitcast.10, bf16[448,512]{1,0:T(8,128)(2,1)} %bitcast.11, bf16[448,512]{1,0:T(8,128)(2,1)} %bitcast.12, ...), custom_call_target="tpu_custom_call" | custom-call | tf_op jit(solution)/shard_map/pallas_call | solution.py:613
  146.1 2.7 %shard_map.121 = (bf16[448,512]{1,0:T(8,128)(2,1)}, bf16[512,128]{1,0:T(8,128)(2,1)}, f32[448,512]{1,0:T(8,128)}, f32[448,512]{1,0:T(8,128)}) custom-call(bf16[448,512]{1,0:T(8,128)(2,1)} %get-tuple-element.12.refs_0_, bf16[512,128]{1,0:T(8,128)(2,1)} %get-tuple-element.13.refs_1_, f32[448,512]{1,0:T(8,128)} %get-tuple-element.14.refs_2_, ...), custom_call_target="tpu_custom_call" | custom-call | tf_op jit(solution)/shard_map/pallas_call | solution.py:623
